TPU v7x, 32 devices: a whole 2x2x4 slice. The times are simulated.
32 devices in a mesh: flow: 8 (over y, x, core), span: 4 (over z).
Axes of the slice: x: 2, y: 2, z: 4, core: 2. Of those that a mesh axis runs over, the one named last changes fastest.
Arguments:
- solid_start: float32 [32, 512, 512], P(None, 'flow', 'span'), may hold values from -6 to 6
- heat_gen: float32 [32, 512, 512], P(None, 'flow', 'span'), may hold values from 0 to 0.05
- conductance: float32 [64, 16384], P('span', 'flow'), may hold values from 0 to 1, as said below
- heat_capacity: float32 [64], P('span'), may hold values from 0.2 to 1
- inlet_temp: float32 [64], P('span'), may hold values from -4 to 4
- wall_owner: int32 [8192, 1], P(('flow', 'span')), may hold values from 0 to 7; in each aligned block of 256 rows (0 to 255, 256 to 511, ...) at most 64 rows name the same one
- wall_row: int32 [8192, 1], P(('flow', 'span')), may hold values from 0 to 63
Outputs:
- solid_final: float32 [32, 512, 512], P(None, 'flow', 'span')
- coolant_final: float32 [64, 16384], P('span', 'flow')
Inputs may be any that keep to these rules, and one draw needn't show every extreme that they name: `conductance`: Positive. `wall_owner`: within the segments of one device (aligned blocks of 256 rows) no flow index is named more than 64 times, and some flow index is named exactly 64 times.
All inputs are finite; a program needn't handle non-finite values.
Results may differ from a plain program's by a relative error of at most 0.0003.
Values sent between devices are 32-bit elements; how exact they have to be, the bound alone decides.
A program may use at most 128 MiB of HBM per device.

v0:
```python
import functools

import jax
import jax.numpy as jnp
from jax import lax
from jax.experimental import pallas as pl
from jax.experimental.pallas import tpu as pltpu
from jax.sharding import PartitionSpec as P

STEPS = 10
KAPPA = 0.16
MESH = pl.DeviceIdType.MESH
F32 = jnp.float32
BF16 = jnp.bfloat16


def split(x):
    hi = x.astype(BF16)
    lo = (x - hi.astype(F32)).astype(BF16)
    return hi, lo


def kernel(dims, cell_ref, cond_ref, lane_ref, start_ref, gen_ref, solid_out, cool_ref,
           field, ring, sides, rows_out, rows_in, cols_out, cols_in,
           decay, gain2, gain4, inner, prefix, factor, temps, own_hot, hot, seg_gain, lane_gain,
           ring_send, ring_recv, side_send, side_recv, row_send, row_recv, col_send, col_recv):
    flow, span, layers, block, seg, channels, count = dims
    width = flow * channels
    cells = flow * block
    group = 2
    me = lax.axis_index("flow")
    at = lax.axis_index("span")
    above, below = at > 0, at < span - 1
    before, after = me > 0, me < flow - 1
    levels = flow.bit_length() - 1

    def ring_copy(slot, hop):
        peer = lax.rem(me + hop, flow)
        return pltpu.make_async_remote_copy(
            src_ref=ring.at[slot, me], dst_ref=ring.at[slot, me],
            send_sem=ring_send.at[hop - 1], recv_sem=ring_recv.at[slot, hop - 1],
            device_id=(peer, at), device_id_type=MESH)

    def side_copy(slot, side):
        return pltpu.make_async_remote_copy(
            src_ref=ring.at[slot, me], dst_ref=sides.at[slot, 1 - side],
            send_sem=side_send.at[side], recv_sem=side_recv.at[slot, 1 - side],
            device_id=(me, at - 1 + 2 * side), device_id_type=MESH)

    def row_copy(slot, side):
        return pltpu.make_async_remote_copy(
            src_ref=rows_out.at[side], dst_ref=rows_in.at[slot, 1 - side],
            send_sem=row_send.at[side], recv_sem=row_recv.at[slot, 1 - side],
            device_id=(me - 1 + 2 * side, at), device_id_type=MESH)

    def col_copy(slot, side):
        return pltpu.make_async_remote_copy(
            src_ref=cols_out, dst_ref=cols_in.at[slot, 1 - side],
            send_sem=col_send.at[side], recv_sem=col_recv.at[slot, 1 - side],
            device_id=(me, at - 1 + 2 * side), device_id_type=MESH)

    def send_bottom(slot):
        for hop in range(1, flow):
            ring_copy(slot, hop).start()
        for side, there in ((0, above), (1, below)):
            @pl.when(there)
            def _():
                side_copy(slot, side).start()

    def sent_bottom(slot):
        for hop in range(1, flow):
            ring_copy(slot, hop).wait_send()
        for side, there in ((0, above), (1, below)):
            @pl.when(there)
            def _():
                side_copy(slot, side).wait_send()

    def arrived_bottom(slot):
        for hop in range(1, flow):
            ring_copy(slot, hop).wait_recv()
        for side, there in ((0, above), (1, below)):
            @pl.when(there)
            def _():
                side_copy(slot, 1 - side).wait_recv()

    def edges(act):
        for side, (in_flow, in_span) in enumerate(((before, above), (after, below))):
            @pl.when(in_flow)
            def _():
                act(row_copy, side)

            @pl.when(in_span)
            def _():
                act(col_copy, side)

    def send_edges(slot):
        edges(lambda copy, side: copy(slot, side).start())

    def sent_edges(slot):
        edges(lambda copy, side: copy(slot, side).wait_send())

    def arrived_edges(slot):
        edges(lambda copy, side: copy(slot, 1 - side).wait_recv())

    sides[...] = jnp.zeros_like(sides)
    rows_in[...] = jnp.zeros_like(rows_in)
    cols_in[...] = jnp.zeros_like(cols_in)
    barrier = pltpu.get_barrier_semaphore()
    for hop in range(1, flow):
        pl.semaphore_signal(barrier, inc=1, device_id=(lax.rem(me + hop, flow), at),
                            device_id_type=MESH)
    for side, there in ((0, above), (1, below)):
        @pl.when(there)
        def _():
            pl.semaphore_signal(barrier, inc=1, device_id=(me, at - 1 + 2 * side),
                                device_id_type=MESH)
    pl.semaphore_wait(barrier, flow - 1 + above.astype(jnp.int32) + below.astype(jnp.int32))

    lane = lax.broadcasted_iota(jnp.int32, (block, seg), 1)
    row = lax.broadcasted_iota(jnp.int32, (block, seg), 0)
    half = seg // 2

    def note_edges(z, new, marks):
        rows_out[0, pl.ds(z, 1), :] = new[0:1, :]
        rows_out[1, pl.ds(z, 1), :] = new[block - 1:block, :]
        marks = jnp.where(lane == z, new[:, 0:1], marks)
        return jnp.where(lane == half + z, new[:, seg - 1:seg], marks)

    ring[0, me] = start_ref[0]
    send_bottom(0)
    marks = jnp.zeros((block, seg), F32)
    rows_out[0, 0:1, :] = jnp.zeros((1, seg), F32)
    rows_out[1, 0:1, :] = jnp.zeros((1, seg), F32)
    field[0, layers] = jnp.zeros((block, seg), F32)
    field[1, layers] = jnp.zeros((block, seg), F32)
    for z in range(1, layers):
        new = start_ref[z]
        field[0, z] = new
        marks = note_edges(z, new, marks)
    cols_out[...] = marks
    send_edges(0)

    nwide = group * width
    place = lax.rem(lax.broadcasted_iota(jnp.int32, (seg, nwide), 0), 8)
    near1, near2, near4 = place >= 1, place >= 2, place >= 4

    def turned(x, k):
        return pltpu.roll(x.reshape(seg // 8, 8, nwide), k, 1).reshape(seg, nwide)

    for pair in range(count // group):
        span_of = pl.ds(pair * nwide, nwide)
        cond = cond_ref[:, span_of]
        d = jnp.exp(-cond)
        decay[:, span_of] = d
        capacity = jnp.concatenate([lane_ref[0:1, :]] * group, axis=1)
        factor[:, span_of] = (jnp.exp(cond) - 1.0) * capacity
        g1 = d * jnp.where(near1, turned(d, 1), 1.0)
        gain2[:, span_of] = jnp.where(near2, g1, 0.0)
        g2 = g1 * jnp.where(near2, turned(g1, 2), 1.0)
        gain4[:, span_of] = jnp.where(near4, g2, 0.0)
        g3 = g2 * jnp.where(near4, turned(g2, 4), 1.0)
        inner[:, span_of] = g3
        enter = jnp.ones((1, nwide), F32)
        for g in range(seg // 8):
            here = g3[8 * g:8 * g + 8] * enter
            prefix[8 * g:8 * g + 8, span_of] = here
            enter = here[7:8]
        target = cell_ref[0:1, span_of]
        mine = target - (me * block).astype(F32)
        own_hot[:, span_of] = (
            lax.broadcasted_iota(jnp.int32, (block, nwide), 0).astype(F32) == mine).astype(BF16)
        if hot is not None:
            hot[:, span_of] = (
                lax.broadcasted_iota(jnp.int32, (cells, nwide), 0).astype(F32) == target
            ).astype(BF16)

    gain = jnp.ones((1, width), F32)
    for t in range(count):
        seg_gain[t:t + 1, :] = gain
        gain = gain * prefix[seg - 1:seg, t * width:(t + 1) * width]
    number = lax.broadcasted_iota(jnp.int32, (1, width), 1) // channels
    for level in range(levels):
        far = number >= (1 << level)
        lane_gain[level:level + 1, :] = jnp.where(far, gain, 0.0)
        gain = gain * jnp.where(far, pltpu.roll(jnp.broadcast_to(gain, (8, width)), channels << level, 1)[0:1], 1.0)
    upper = jnp.where(number >= 1, pltpu.roll(jnp.broadcast_to(gain, (8, width)), channels, 1)[0:1], 1.0)
    lane_gain[levels:levels + 1, :] = upper * lane_ref[1:2, :]

    def roll_lanes(x, k):
        return pltpu.roll(jnp.broadcast_to(x, (8, width)), k, 1)[0:1]

    def around(c, low_row, high_row, low_col, high_col):
        beside = jnp.where(row == 0, low_row, pltpu.roll(c, 1, 0))
        beside = beside + jnp.where(row == block - 1, high_row, pltpu.roll(c, block - 1, 0))
        beside = beside + jnp.where(lane == 0, low_col, pltpu.roll(c, 1, 1))
        return beside + jnp.where(lane == seg - 1, high_col, pltpu.roll(c, seg - 1, 1))

    def step(turn, carry):
        slot, later = lax.rem(turn, 2), lax.rem(turn + 1, 2)
        arrived_bottom(slot)
        sent_bottom(slot)
        base = ring[slot].reshape(cells, seg)
        hi, lo = split(base.T)
        lhs = jnp.concatenate([hi, lo], axis=0)
        for pair in range(count // group):
            span_of = pl.ds(pair * nwide, nwide)
            if hot is not None:
                picked = jnp.dot(lhs, hot[:, span_of], preferred_element_type=F32)
            else:
                picked = jnp.zeros((2 * seg, nwide), F32)
                part = min(cells, 512)
                for first in range(0, cells, part):
                    one = (lax.broadcasted_iota(jnp.int32, (part, nwide), 0) + first).astype(F32)
                    one = (one == cell_ref[0:1, span_of]).astype(BF16)
                    picked += jnp.dot(lhs[:, first:first + part], one, preferred_element_type=F32)
            w = picked[:seg] + picked[seg:]
            temps[:, span_of] = w
            d = decay[:, span_of]
            s = w - d * w
            s = s + jnp.where(near1, d, 0.0) * turned(s, 1)
            s = s + gain2[:, span_of] * turned(s, 2)
            s = s + gain4[:, span_of] * turned(s, 4)
            cool_ref[:, span_of] = s
        for t in range(count):
            span_of = pl.ds(t * width, width)
            enter = jnp.zeros((1, width), F32)
            for g in range(seg // 8):
                here = pl.ds(8 * g, 8)
                local = cool_ref[here, span_of]
                if g:
                    local = local + inner[here, span_of] * enter
                    cool_ref[here, span_of] = local
                enter = local[7:8]
        run = jnp.zeros((1, width), F32)
        runs = []
        for t in range(count):
            runs.append(run)
            whole = pl.ds(t * width, width)
            run = prefix[seg - 1:seg, whole] * run + cool_ref[seg - 1:seg, whole]
        for level in range(levels):
            run = run + lane_gain[level:level + 1, :] * roll_lanes(run, channels << level)
        carry_in = jnp.where(number >= 1, roll_lanes(run, channels), 0.0) + lane_gain[levels:levels + 1, :]
        sink = jnp.zeros((block, 2 * seg), F32)
        for pair in range(count // group):
            span_of = pl.ds(pair * nwide, nwide)
            enter = jnp.concatenate(
                [runs[t] + seg_gain[t:t + 1, :] * carry_in
                 for t in range(pair * group, (pair + 1) * group)], axis=1)
            coolant = cool_ref[:, span_of] + prefix[:, span_of] * enter
            cool_ref[:, span_of] = coolant
            heat = factor[:, span_of] * (temps[:, span_of] - coolant)
            hi, lo = split(heat)
            sink = sink + lax.dot_general(
                own_hot[:, span_of], jnp.concatenate([hi, lo], axis=0),
                (((1,), (1,)), ((), ())), preferred_element_type=F32)
        sink = sink[:, :seg] + sink[:, seg:]
        c = ring[slot, me]
        low = ring[slot, jnp.maximum(me - 1, 0), block - 1:block, :]
        high = ring[slot, jnp.minimum(me + 1, flow - 1), 0:1, :]
        low = jnp.where(before, low, 0.0)
        high = jnp.where(after, high, 0.0)
        beside = around(c, low, high, sides[slot, 0][:, seg - 1:seg], sides[slot, 1][:, 0:1])
        beside = beside + field[slot, 1]
        bottom = c + KAPPA * (beside - 6.0 * c) + gen_ref[0] - sink
        ring[later, me] = bottom
        solid_out[0] = bottom

        @pl.when(turn < STEPS - 1)
        def _():
            send_bottom(later)

        arrived_edges(slot)
        sent_edges(slot)
        marks = jnp.zeros((block, seg), F32)
        low_cols = cols_in[slot, 0]
        high_cols = cols_in[slot, 1]
        for z in range(1, layers):
            c = field[slot, z]
            beside = around(c, rows_in[slot, 0, z:z + 1, :], rows_in[slot, 1, z:z + 1, :],
                            low_cols[:, half + z:half + z + 1], high_cols[:, z:z + 1])
            under = ring[slot, me] if z == 1 else field[slot, z - 1]
            beside = beside + under + field[slot, z + 1]
            new = c + KAPPA * (beside - 6.0 * c) + gen_ref[z]
            field[later, z] = new
            marks = note_edges(z, new, marks)
        cols_out[...] = marks

        @pl.when(turn < STEPS - 1)
        def _():
            send_edges(later)
        return carry

    lax.fori_loop(0, STEPS, step, 0)
    last = STEPS % 2
    for z in range(1, layers):
        solid_out[z] = field[last, z]


def body(solid_start, heat_gen, conductance, heat_capacity, inlet_temp, wall_owner, wall_row):
    flow = lax.axis_size("flow")
    span = lax.axis_size("span")
    layers, block, seg = solid_start.shape
    channels, stations = conductance.shape
    count = stations // seg
    segs = channels * count
    me = lax.axis_index("flow")
    cell = (wall_owner[:, 0] * block + wall_row[:, 0]).astype(F32).reshape(segs // seg, seg)
    packed = jnp.concatenate([conductance.reshape(segs, seg), cell], axis=0)
    packed = lax.all_gather(packed, "flow")
    cond = packed[:, :segs].reshape(flow, channels, count, seg)
    cond = jnp.transpose(cond, (3, 2, 0, 1)).reshape(seg, count * flow * channels)
    cell = packed[:, segs:].reshape(flow, channels, count)
    cell = jnp.transpose(cell, (2, 0, 1)).reshape(1, count * flow * channels)
    per_lane = jnp.stack([jnp.tile(heat_capacity, flow), jnp.tile(inlet_temp, flow)])
    width = flow * channels
    total = count * width
    keep = flow * block * total * 2 <= (8 << 20)
    dims = (flow, span, layers, block, seg, channels, count)
    vm = pltpu.VMEM
    dma = pltpu.SemaphoreType.DMA
    big = vm((seg, total), F32)
    scratch = [
        vm((2, layers + 1, block, seg), F32), vm((2, flow, block, seg), F32),
        vm((2, 2, block, seg), F32), vm((2, layers, seg), F32), vm((2, 2, layers, seg), F32),
        vm((block, seg), F32), vm((2, 2, block, seg), F32),
        big, big, big, big, big, big, big, vm((block, total), BF16),
    ]
    if keep:
        scratch.append(vm((flow * block, total), BF16))
    scratch += [
        vm((count, width), F32), vm((8, width), F32),
        dma((flow - 1,)), dma((2, flow - 1)), dma((2,)), dma((2, 2)),
        dma((2,)), dma((2, 2)), dma((2,)), dma((2, 2)),
    ]

    def run(*refs):
        if not keep:
            refs = refs[:22] + (None,) + refs[22:]
        kernel(dims, *refs)

    solid, cool = pl.pallas_call(
        run,
        out_shape=(jax.ShapeDtypeStruct(solid_start.shape, F32),
                   jax.ShapeDtypeStruct((seg, total), F32)),
        in_specs=[pl.BlockSpec(memory_space=pltpu.VMEM)] * 5,
        out_specs=(pl.BlockSpec(memory_space=pltpu.VMEM),) * 2,
        scratch_shapes=scratch,
        compiler_params=pltpu.CompilerParams(
            collective_id=0, has_side_effects=True, vmem_limit_bytes=60 << 20),
    )(cell, cond, per_lane, solid_start, heat_gen)
    cool = cool.reshape(seg, count, flow, channels)
    cool = lax.dynamic_index_in_dim(cool, me, 2, False)
    return solid, jnp.transpose(cool, (2, 1, 0)).reshape(channels, stations)


def solution(mesh):
    placed = (
        P(None, "flow", "span"),
        P(None, "flow", "span"),
        P("span", "flow"),
        P("span"),
        P("span"),
        P(("flow", "span"), None),
        P(("flow", "span"), None),
    )
    return jax.shard_map(
        body,
        mesh=mesh,
        in_specs=placed,
        out_specs=(P(None, "flow", "span"), P("span", "flow")),
        check_vma=False,
    )
```

profile of v0, /device:TPU:0, one launch (start us, length us, event | category | flops | bytes accessed | tf_op | source)
XLA Modules:
  0.0 132.1 jit_solution(8913531005460205682)
XLA Ops:
  7.2 0.0 all-gather.4.cloned.1.call-start
  7.2 0.9 reshape.34
  8.1 0.7 add_convert_fusion
  8.8 0.7 maximum_bitcast_fusion
  9.5 0.0 all-gather.4.cloned.1.call-update
  9.5 0.7 tile.5
  10.2 0.1 stack_tile.7
  10.3 0.7 tile.4
  10.9 0.1 stack_tile.6
  11.0 0.6 pad_maximum_fusion.refs_2_
  11.6 25.1 %all-gather.4.cloned.1.call-done = f32[8,258,128]{2,1,0:T(8,128)} async-done(((f32[1,258,128]{2,1,0:T(8,128)}), f32[8,258,128]{2,1,0:T(8,128)}) %all-gather.4.cloned.1.call-update) | async-done | bytes 1056784 | tf_op jit(solution)/shard_map/all_gather | solution.py:309
  36.7 0.8 slice.8
  37.5 0.1 reshape.35
  37.5 0.1 copy.18
  37.6 0.0 slice-start
  37.7 0.7 reshape.36.refs_0_
  38.3 0.5 slice-done
  38.9 0.3 copy.19
  39.2 1.3 copy.20.refs_1_
  40.5 81.4 %shard_map.86 = (f32[32,64,128]{2,1,0:T(8,128)}, f32[128,2048]{1,0:T(8,128)}) custom-call(f32[1,2048]{1,0:T(1,128)} %reshape.36.refs_0_, f32[128,2048]{1,0:T(8,128)} %copy.20.refs_1_, f32[2,128]{1,0:T(2,128)} %pad_maximum_fusion.refs_2_, f32[32,64,128]{2,1,0:T(8,128)} %refs_3_.1, f32[32,64,128]{2,1,0:T(8,128)} %refs_4_.1), custom_call_target="tpu_custom_call" | custom-call | tf_op jit(solution)/shard_map/pallas_call | solution.py:341
  121.9 0.0 copy-start
  121.9 1.6 %copy.21 = f32[128,2048]{0,1:T(8,128)S(1)} copy(f32[128,2048]{1,0:T(8,128)} %get-tuple-element.5) | data formatting | bytes 2097152 | tf_op jit(solution)/shard_map/pallas_call | solution.py:341
  123.6 0.7 copy_bitcast_fusion
  124.2 1.0 copy.26
  (1 shorter events, 0.0 us)
Async XLA Ops:
  7.2 29.5 %all-gather.4.cloned.1.call-start = ((), (), s32[]{:S(2)}) async-start(), calls=%async_computation | async-start | bytes 1216512 | tf_op jit(solution)/shard_map/all_gather | solution.py:309
  37.6 1.2 slice-start
  121.9 2.3 %copy-start = (f32[32,64,128]{2,1,0:T(8,128)S(1)}, f32[32,64,128]{2,1,0:T(8,128)}, u32[]{:S(2)}) copy-start(f32[32,64,128]{2,1,0:T(8,128)} %get-tuple-element.8) | copy-start | bytes 3145732
Sparse Core Ops, SparseCore 0:
  10.4 26.2 all-gather.3
where the time goes:
time: 132 us
  Pallas kernels  81.4 us (62%)
  waiting for transfers between devices  25.1 us (19%)
  between operations  14.1 us (11%)
  local copies, waits for them, and re-layouts  9.5 us (7%)
  other arithmetic  1.96 us (1%)
    pallas_call x1, Pallas kernels, body(): pl.pallas_call(run, out_shape=(jax.ShapeDtypeStruct(solid_start.shape, F3...  81.4 us
    all_gather x1, waiting for transfers between devices, body(): packed = lax.all_gather(packed, 'flow')  25.1 us
  transfers between devices with their start and end apart: 1, of which 1 were waited for; matrix products, arithmetic and copies ran while one was open for 2% of the time, Pallas kernels for 0%

commit v1 on v0

v1 whole, which is shorter than its diff:
```python
import jax
import jax.numpy as jnp
from jax import lax
from jax.experimental import pallas as pl
from jax.experimental.pallas import tpu as pltpu
from jax.sharding import PartitionSpec as P

STEPS = 10
KAPPA = 0.16
MESH = pl.DeviceIdType.MESH
F32 = jnp.float32
BF16 = jnp.bfloat16


def split(x):
    hi = x.astype(BF16)
    lo = (x - hi.astype(F32)).astype(BF16)
    return hi, lo


def kernel(dims, owner_ref, row_ref, cap_ref, inlet_ref, cond_ref, start_ref, gen_ref,
           solid_out, cool_out, s):
    flow, span, layers, block, seg, channels, count, group, keep = dims
    width = flow * channels
    cells = flow * block
    half = flow // 2
    tiles = block // 8
    lines = cells // 8
    packs = -(-lines // (seg // 2))
    me = lax.axis_index("flow")
    at = lax.axis_index("span")
    mate = me + 1 - 2 * lax.rem(me, 2)
    above, below = at > 0, at < span - 1
    before, after = me > 0, me < flow - 1

    lane = lax.broadcasted_iota(jnp.int32, (8, seg), 1)
    pair = lane // 2
    lane_b = lax.broadcasted_iota(jnp.int32, (block, seg), 1)
    row_b = lax.broadcasted_iota(jnp.int32, (block, seg), 0)
    first_b, last_b = lane_b == 0, lane_b == seg - 1
    top_b, low_b = row_b == 0, row_b == block - 1

    def remote(src, dst, send, recv, device):
        return pltpu.make_async_remote_copy(
            src_ref=src, dst_ref=dst, send_sem=send, recv_sem=recv,
            device_id=device, device_id_type=MESH)

    kinds = (
        (s.idx_own, lambda f: s.idx.at[f]),
        (start_ref.at[pl.ds(0, 2)], lambda f: s.first.at[f]),
        (cond_ref, lambda f: s.gain.at[f]),
        (gen_ref.at[0], lambda f: s.gen0.at[f]),
    )

    def direct(kind, hop):
        src, dst = kinds[kind]
        to = lax.rem(me + 2 * hop, flow)
        return remote(src, dst(me), s.once_send.at[kind, 2 * hop - 1], s.once_recv.at[kind, 2 * hop - 1], (to, at))

    def to_mate(kind):
        src, dst = kinds[kind]
        return remote(src, dst(me), s.once_send.at[kind, 0], s.once_recv.at[kind, 0], (mate, at))

    def relay(kind, hop):
        _, dst = kinds[kind]
        origin = lax.rem(me + flow - 2 * hop, flow)
        return remote(dst(origin), dst(origin), s.once_send.at[kind, 2 * hop], s.once_recv.at[kind, 2 * hop], (mate, at))

    def layer_copy(slot, hop):
        peer = lax.rem(me + hop, flow)
        return remote(s.one.at[slot, me], s.one.at[slot, me],
                      s.one_send.at[hop - 1], s.one_recv.at[slot, hop - 1], (peer, at))

    def side_copy(slot, side):
        return remote(s.side_out, s.side_in.at[slot, 1 - side],
                      s.side_send.at[side], s.side_recv.at[slot, 1 - side], (me, at - 1 + 2 * side))

    def rim_copy(slot, side):
        return remote(s.rim_out, s.rim_in.at[slot, 1 - side],
                      s.rim_send.at[side], s.rim_recv.at[slot, 1 - side], (me, at - 1 + 2 * side))

    def col_copy(slot, side):
        return remote(s.col_out, s.col_in.at[slot, 1 - side],
                      s.col_send.at[side], s.col_recv.at[slot, 1 - side], (me, at - 1 + 2 * side))

    def row_copy(slot, side):
        return remote(s.row_out.at[side], s.row_in.at[slot, 1 - side],
                      s.row_send.at[side], s.row_recv.at[slot, 1 - side], (me - 1 + 2 * side, at))

    def both(copy, pair_of, act):
        for side, there in enumerate(pair_of):
            @pl.when(there)
            def _():
                act(copy, side)

    in_span, in_flow = (above, below), (before, after)

    def start(copy, slot, pair_of):
        both(copy, pair_of, lambda c, side: c(slot, side).start())

    def sent(copy, slot, pair_of):
        both(copy, pair_of, lambda c, side: c(slot, side).wait_send())

    def arrived(copy, slot, pair_of):
        both(copy, pair_of, lambda c, side: c(slot, 1 - side).wait_recv())

    s.side_in[...] = jnp.zeros_like(s.side_in)
    s.rim_in[...] = jnp.zeros_like(s.rim_in)
    s.col_in[...] = jnp.zeros_like(s.col_in)
    s.row_in[...] = jnp.zeros_like(s.row_in)
    s.idx_own[...] = jnp.zeros_like(s.idx_own)
    per = owner_ref.shape[0]
    s.idx_own[0:per, :] = owner_ref[...].astype(F32)
    s.idx_own[per:2 * per, :] = row_ref[...].astype(F32)
    barrier = pltpu.get_barrier_semaphore()
    for hop in range(1, flow):
        pl.semaphore_signal(barrier, inc=1, device_id=(lax.rem(me + hop, flow), at), device_id_type=MESH)
    for side, there in enumerate(in_span):
        @pl.when(there)
        def _():
            pl.semaphore_signal(barrier, inc=1, device_id=(me, at - 1 + 2 * side), device_id_type=MESH)
    pl.semaphore_wait(barrier, flow - 1 + above.astype(jnp.int32) + below.astype(jnp.int32))
    for kind in range(len(kinds)):
        for hop in range(1, half):
            direct(kind, hop).start()
        to_mate(kind).start()
    s.idx[me] = s.idx_own[...]
    s.first[me] = start_ref[0:2]
    s.gain[me] = cond_ref[...]
    s.gen0[me] = gen_ref[0]

    def packed(marks, value, place):
        for r in range(tiles):
            p, k = place(r)
            turned = pltpu.roll(value[8 * r:8 * r + 8], 2 * k + 1, 1)
            marks[p] = jnp.where(pair == k, turned, marks[p])
        return marks

    def merged(low, high):
        return jnp.where(lax.rem(lane, 2) == 0, pltpu.roll(high, seg - 1, 1), pltpu.roll(low, 1, 1))

    def unpacked(marks, place):
        return jnp.concatenate(
            [pltpu.roll(marks[p], seg - 1 - 2 * k, 1) for p, k in (place(r) for r in range(tiles))], axis=0)

    def rim_place(r):
        return 0, r

    def col_place(z):
        per_pack = seg // 2 // layers
        return lambda r: (r // per_pack, z + layers * (r % per_pack))

    def side_place(b):
        return lambda r: divmod(b * tiles + r, seg // 2)

    col_packs = s.col_out.shape[0]
    empty = jnp.zeros((8, seg), F32)

    def around(c, low_row, high_row, halo):
        beside = jnp.where(top_b, low_row, pltpu.roll(c, 1, 0))
        beside = beside + jnp.where(low_b, high_row, pltpu.roll(c, block - 1, 0))
        beside = beside + jnp.where(first_b, halo, pltpu.roll(c, 1, 1))
        return beside + jnp.where(last_b, halo, pltpu.roll(c, seg - 1, 1))

    marks = [empty] * col_packs
    for side in range(2):
        s.row_out[side] = jnp.zeros_like(s.row_out[side])
    s.field[0, layers] = jnp.zeros((block, seg), F32)
    s.field[1, layers] = jnp.zeros((block, seg), F32)

    def note_rows(z, new):
        s.row_out[0, z:z + 1, :] = new[0:1, :]
        s.row_out[1, z:z + 1, :] = new[block - 1:block, :]

    new = start_ref[1]
    s.field[0, 1] = new
    s.rim_out[...] = packed([empty], new, rim_place)[0]
    start(rim_copy, 0, in_span)
    for z in range(2, layers):
        new = start_ref[z]
        s.field[0, z] = new
        note_rows(z, new)
        marks = packed(marks, new, col_place(z))
    for p in range(col_packs):
        s.col_out[p] = marks[p]
    start(row_copy, 0, in_flow)
    start(col_copy, 0, in_span)

    mid = seg // 2 - 1
    i2 = lax.rem(lax.broadcasted_iota(jnp.int32, (2 * seg, 2 * seg), 0), seg)
    j2 = lax.broadcasted_iota(jnp.int32, (2 * seg, 2 * seg), 1)
    tri = jnp.where((i2 <= j2) | (j2 >= seg), 1.0, 0.0).astype(BF16)
    s.tri[...] = tri
    i3 = lax.rem(lax.broadcasted_iota(jnp.int32, (3 * seg, 3 * seg), 0), seg)
    j3 = lax.broadcasted_iota(jnp.int32, (3 * seg, 3 * seg), 1)
    lower = jnp.where(i3 <= mid, 1.0, 0.0)
    spread = jnp.where(j3 < seg, jnp.where(i3 <= j3, 1.0, 0.0) - lower,
                       jnp.where(j3 < 2 * seg, lower, 1.0 - lower)).astype(BF16)
    eye = (lax.broadcasted_iota(jnp.int32, (channels, channels), 0)
           == lax.broadcasted_iota(jnp.int32, (channels, channels), 1))

    def column(ref):
        wide = jnp.where(eye, jnp.broadcast_to(ref[...], (channels, channels)), 0.0)
        return jnp.broadcast_to(jnp.sum(wide, axis=1, keepdims=True), (channels, seg))

    capacity, inlet = column(cap_ref), column(inlet_ref)

    def arrivals(kind, i):
        hop = i // 2
        odd = lax.rem(i, 2) == 1

        @pl.when(jnp.logical_and(jnp.logical_not(odd), i > 0))
        def _():
            direct(kind, hop).wait_recv()
            relay(kind, hop).start()

        @pl.when(i == 1)
        def _():
            to_mate(kind).wait_recv()

        @pl.when(jnp.logical_and(odd, i > 1))
        def _():
            relay(kind, hop).wait_recv()

    def gather_kind(kind):
        def body(i, carry):
            arrivals(kind, i)
            return carry
        lax.fori_loop(0, flow, body, 0)

    gather_kind(0)
    share = seg // count
    lane_i = lax.broadcasted_iota(jnp.int32, (channels, seg), 1) // count
    chan_i = lax.rem(lax.broadcasted_iota(jnp.int32, (channels, seg), 0), share)
    here = lane_i == chan_i

    def one_source(f, carry):
        def taken(base):
            rows = jnp.concatenate(
                [jnp.broadcast_to(s.idx[f, base + a:base + a + 1, :], (share, seg)) for a in range(per)], axis=0)
            return jnp.where(here, rows, 0.0).astype(BF16)
        s.seats[f] = jnp.concatenate([taken(0), taken(per)], axis=1)
        return carry

    lax.fori_loop(0, flow, one_source, 0)
    seats = s.seats[...].reshape(width, 2 * seg)
    ci = lax.broadcasted_iota(jnp.int32, (2 * seg, seg), 0)
    weight = jnp.where(ci < seg, float(block), 1.0)
    turn_of = lax.rem(ci, count)
    ri = lax.broadcasted_iota(jnp.int32, (count, 2 * seg), 1)
    rt = lax.broadcasted_iota(jnp.int32, (count, 2 * seg), 0)
    pick = jnp.where(lax.rem(ri, count) == rt, jnp.where(ri < seg, float(block), 1.0), 0.0).astype(BF16)
    s.along[...] = lax.dot_general(pick, seats, (((1,), (1,)), ((), ())), preferred_element_type=F32)

    def one_turn(t, carry):
        chosen = jnp.where(turn_of == t, weight, 0.0).astype(BF16)
        cell = jnp.dot(seats, chosen, preferred_element_type=F32)
        if keep:
            lanes = lax.broadcasted_iota(jnp.int32, (width, seg), 1).astype(F32)
            rows = pl.ds(pl.multiple_of(t * width, width), width)
            for k in range(cells // seg):
                s.take[rows, k * seg:(k + 1) * seg] = jnp.where(cell - float(k * seg) == lanes, 1.0, 0.0).astype(BF16)
        else:
            s.take[t] = cell
        return carry

    lax.fori_loop(0, count, one_turn, 0)
    if keep:
        for t in range(count):
            for b in range(flow):
                rows = lax.broadcasted_iota(jnp.int32, (block, width), 0).astype(F32) + float(b * block)
                s.give[b * block:(b + 1) * block, t * width:(t + 1) * width] = jnp.where(
                    rows == s.along[t:t + 1, :], 1.0, 0.0).astype(BF16)

    def take_rows(t0):
        if keep:
            return s.take[t0 * width:(t0 + group) * width, :]
        cell = s.take[t0:t0 + group].reshape(group * width, seg)
        lanes = lax.broadcasted_iota(jnp.int32, (group * width, seg), 1).astype(F32)
        return jnp.concatenate(
            [jnp.where(cell - float(k * seg) == lanes, 1.0, 0.0).astype(BF16) for k in range(cells // seg)], axis=1)

    def give_rows(t0, b):
        if keep:
            return s.give[b * block:(b + 1) * block, t0 * width:(t0 + group) * width]
        rows = lax.broadcasted_iota(jnp.int32, (block, width), 0).astype(F32) + float(b * block)
        return jnp.concatenate(
            [jnp.where(rows == s.along[t:t + 1, :], 1.0, 0.0).astype(BF16) for t in range(t0, t0 + group)], axis=1)

    gather_kind(1)

    def place_first(f, carry):
        s.plane[0, f] = s.first[f, 0]
        s.one[0, f] = s.first[f, 1]
        return carry

    lax.fori_loop(0, flow, place_first, 0)
    side_marks = [empty] * packs
    for b in range(flow):
        c = s.plane[0, b]
        side_marks = packed(side_marks, c, side_place(b))
        hi, lo = split(c)
        s.base[b * block:(b + 1) * block, 0:seg] = hi
        s.base[b * block:(b + 1) * block, seg:2 * seg] = lo
    for p in range(packs):
        s.side_out[p] = side_marks[p]
    start(side_copy, 0, in_span)

    def chunk(ref, t):
        return ref[:, :, t * seg:(t + 1) * seg].reshape(width, seg)

    def constants(i, carry):
        arrivals(2, i)
        hop = i // 2
        from_me = lax.rem(me + flow - 2 * hop, flow)
        from_mate = lax.rem(mate + flow - 2 * hop, flow)
        f = jnp.where(lax.rem(i, 2) == 0, from_me, from_mate)

        @pl.when(jnp.logical_and(lax.rem(i, 2) == 0, i > 0))
        def _():
            relay(2, hop).wait_send()

        k = jnp.concatenate([s.gain[f, :, t * seg:(t + 1) * seg] for t in range(count)], axis=0)
        k1 = k.astype(BF16)
        rest = k - k1.astype(F32)
        k2 = rest.astype(BF16)
        k3 = (rest - k2.astype(F32)).astype(BF16)
        sums = jnp.dot(jnp.concatenate([k1, k2, k3], axis=1), spread, preferred_element_type=F32)
        run = jnp.ones((channels, seg), F32)
        for t in range(count):
            rows = slice(t * channels, (t + 1) * channels)
            cols = slice(t * seg, (t + 1) * seg)
            kt, depth = k[rows], sums[rows, 0:seg]
            fore, rear = jnp.exp(-sums[rows, seg:2 * seg]), jnp.exp(-sums[rows, 2 * seg:])
            s.gain[f, :, cols] = (1.0 - jnp.exp(-kt)) * jnp.exp(depth)
            s.fall[f, :, cols] = jnp.exp(-depth)
            s.heat_of[f, :, cols] = (jnp.exp(kt) - 1.0) * capacity
            s.fore[f, :, cols] = fore
            s.rear[f, :, cols] = rear
            s.reach[f, :, cols] = run
            run = run * (fore * rear)
        s.whole[f] = run
        return carry

    lax.fori_loop(0, flow, constants, 0)
    gather_kind(3)

    def coolant():
        base = s.base[...]
        run = jnp.zeros((width, seg), F32)
        for t0 in range(0, count, group):
            found = jnp.dot(take_rows(t0), base, preferred_element_type=F32)
            w = found[:, :seg] + found[:, seg:]
            gains = jnp.concatenate([chunk(s.gain, t) for t in range(t0, t0 + group)], axis=0)
            hi, lo = split(gains * w)
            sums = jnp.dot(jnp.concatenate([hi, lo], axis=1), s.tri[...], preferred_element_type=F32)
            for i in range(group):
                t = t0 + i
                rows = slice(i * width, (i + 1) * width)
                s.wall[t] = w[rows]
                s.part[t] = sums[rows, :seg]
                s.run[t] = run
                run = chunk(s.rear, t) * (sums[rows, seg:] + chunk(s.fore, t) * run)
        enter = inlet
        for f in range(flow):
            s.enter[f] = enter
            enter = run[f * channels:(f + 1) * channels] + s.whole[f] * enter
        enter = s.enter[...].reshape(width, seg)
        for t0 in range(0, count, group):
            for t in range(t0, t0 + group):
                first = s.run[t] + chunk(s.reach, t) * enter
                cool = chunk(s.fall, t) * (s.part[t] + chunk(s.fore, t) * first)
                hi, lo = split(chunk(s.heat_of, t) * (s.wall[t] - cool))
                s.heat[t * width:(t + 1) * width, 0:seg] = hi
                s.heat[t * width:(t + 1) * width, seg:2 * seg] = lo

    def sinks(b):
        total = jnp.zeros((block, 2 * seg), F32)
        for t0 in range(0, count, group):
            total = total + jnp.dot(give_rows(t0, b), s.heat[t0 * width:(t0 + group) * width, :],
                                    preferred_element_type=F32)
        return total[:, :seg] + total[:, seg:]

    def step(turn, carry):
        slot, later = lax.rem(turn, 2), lax.rem(turn + 1, 2)
        held, next_held = lax.rem(turn, 4), lax.rem(turn + 1, 4)
        more = turn < STEPS - 1

        @pl.when(turn > 0)
        def _():
            layer_copy(held, 1).wait_recv()
            if flow > 2:
                layer_copy(held, flow - 1).wait_recv()
            for hop in range(1, flow):
                layer_copy(held, hop).wait_send()
        arrived(rim_copy, slot, in_span)
        sent(rim_copy, slot, in_span)
        c = s.field[slot, 1]
        low = s.one[held, jnp.maximum(me - 1, 0), block - 1:block, :]
        high = s.one[held, jnp.minimum(me + 1, flow - 1), 0:1, :]
        halo = unpacked([merged(s.rim_in[slot, 0], s.rim_in[slot, 1])], rim_place)
        beside = around(c, jnp.where(before, low, 0.0), jnp.where(after, high, 0.0), halo)
        beside = beside + s.plane[slot, me] + s.field[slot, 2]
        new = c + KAPPA * (beside - 6.0 * c) + gen_ref[1]
        s.field[later, 1] = new
        s.one[next_held, me] = new
        s.rim_out[...] = packed([empty], new, rim_place)[0]

        @pl.when(more)
        def _():
            for hop in range(1, flow):
                layer_copy(next_held, hop).start()
        @pl.when(more)
        def _():
            start(rim_copy, later, in_span)

        coolant()

        arrived(row_copy, slot, in_flow)
        sent(row_copy, slot, in_flow)
        arrived(col_copy, slot, in_span)
        sent(col_copy, slot, in_span)
        marks = [empty] * col_packs
        halos = [merged(s.col_in[slot, 0, p], s.col_in[slot, 1, p]) for p in range(col_packs)]
        for z in range(2, layers):
            c = s.field[slot, z]
            beside = around(c, s.row_in[slot, 0, z:z + 1, :], s.row_in[slot, 1, z:z + 1, :],
                            unpacked(halos, col_place(z)))
            beside = beside + s.field[slot, z - 1] + s.field[slot, z + 1]
            new = c + KAPPA * (beside - 6.0 * c) + gen_ref[z]
            s.field[later, z] = new
            note_rows(z, new)
            marks = packed(marks, new, col_place(z))
        for p in range(col_packs):
            s.col_out[p] = marks[p]

        @pl.when(more)
        def _():
            start(row_copy, later, in_flow)
            start(col_copy, later, in_span)

        @pl.when(turn > 0)
        def _():
            for hop in range(2, flow - 1):
                layer_copy(held, hop).wait_recv()
        arrived(side_copy, slot, in_span)
        sent(side_copy, slot, in_span)
        halos = [merged(s.side_in[slot, 0, p], s.side_in[slot, 1, p]) for p in range(packs)]
        side_marks = [empty] * packs
        for b in range(flow):
            c = s.plane[slot, b]
            low = s.plane[slot, b - 1, block - 1:block, :] if b else jnp.zeros((1, seg), F32)
            high = s.plane[slot, b + 1, 0:1, :] if b < flow - 1 else jnp.zeros((1, seg), F32)
            beside = around(c, low, high, unpacked(halos, side_place(b))) + s.one[held, b]
            new = c + KAPPA * (beside - 6.0 * c) + s.gen0[b] - sinks(b)
            s.plane[later, b] = new
            side_marks = packed(side_marks, new, side_place(b))
            hi, lo = split(new)
            s.base[b * block:(b + 1) * block, 0:seg] = hi
            s.base[b * block:(b + 1) * block, seg:2 * seg] = lo
        for p in range(packs):
            s.side_out[p] = side_marks[p]

        @pl.when(more)
        def _():
            start(side_copy, later, in_span)
        return carry

    lax.fori_loop(0, STEPS, step, 0)
    for kind in range(len(kinds)):
        for hop in range(1, half):
            direct(kind, hop).wait_send()
            if kind != 2:
                relay(kind, hop).wait_send()
        to_mate(kind).wait_send()
    last = STEPS % 2
    solid_out[0] = s.plane[last, me]
    for z in range(1, layers):
        solid_out[z] = s.field[last, z]
    rows = pl.ds(pl.multiple_of(me * channels, channels), channels)
    for t in range(count):
        cols = slice(t * seg, (t + 1) * seg)
        first = s.run[t, rows, :] + s.reach[me, :, cols] * s.enter[me]
        cool_out[:, cols] = s.fall[me, :, cols] * (s.part[t, rows, :] + s.fore[me, :, cols] * first)


class Scratch:
    pass


def body(solid_start, heat_gen, conductance, heat_capacity, inlet_temp, wall_owner, wall_row):
    flow = lax.axis_size("flow")
    span = lax.axis_size("span")
    layers, block, seg = solid_start.shape
    channels, stations = conductance.shape
    count = stations // seg
    segs = channels * count
    width = flow * channels
    total = count * width
    cells = flow * block
    half = flow // 2
    lines = cells // 8
    keep = cells * total * 4 <= (8 << 20)
    group = max(1, 512 // width)
    packs = -(-lines // (seg // 2))
    col_packs = -(-(block // 8) // (seg // 2 // layers))
    dims = (flow, span, layers, block, seg, channels, count, group, keep)
    vm = pltpu.VMEM
    dma = pltpu.SemaphoreType.DMA
    march = vm((flow, channels, stations), F32)
    parts = vm((count, width, seg), F32)
    scratch = dict(
        idx_own=vm((8, seg), F32), idx=vm((flow, 8, seg), F32), first=vm((flow, 2, block, seg), F32),
        gen0=vm((flow, block, seg), F32), one=vm((4, flow, block, seg), F32),
        plane=vm((2, flow, block, seg), F32), field=vm((2, layers + 1, block, seg), F32),
        side_out=vm((packs, 8, seg), F32), side_in=vm((2, 2, packs, 8, seg), F32),
        rim_out=vm((8, seg), F32), rim_in=vm((2, 2, 8, seg), F32),
        col_out=vm((col_packs, 8, seg), F32), col_in=vm((2, 2, col_packs, 8, seg), F32),
        row_out=vm((2, layers, seg), F32), row_in=vm((2, 2, layers, seg), F32),
        tri=vm((2 * seg, 2 * seg), BF16), seats=vm((flow, channels, 2 * seg), BF16),
        along=vm((count, width), F32),
        take=vm((total, cells), BF16) if keep else parts,
        base=vm((cells, 2 * seg), BF16), heat=vm((total, 2 * seg), BF16),
        gain=march, fall=march, heat_of=march, fore=march, rear=march, reach=march,
        whole=vm((flow, channels, seg), F32), enter=vm((flow, channels, seg), F32),
        wall=parts, part=parts, run=parts,
        once_send=dma((4, flow - 1)), once_recv=dma((4, flow - 1)),
        one_send=dma((flow - 1,)), one_recv=dma((4, flow - 1)),
        side_send=dma((2,)), side_recv=dma((2, 2)), rim_send=dma((2,)), rim_recv=dma((2, 2)),
        col_send=dma((2,)), col_recv=dma((2, 2)), row_send=dma((2,)), row_recv=dma((2, 2)),
    )
    if keep:
        scratch["give"] = vm((cells, total), BF16)
    names = list(scratch)

    def run(*refs):
        held = Scratch()
        for name, ref in zip(names, refs[9:]):
            setattr(held, name, ref)
        kernel(dims, *refs[:9], held)

    return pl.pallas_call(
        run,
        out_shape=(jax.ShapeDtypeStruct(solid_start.shape, F32),
                   jax.ShapeDtypeStruct(conductance.shape, F32)),
        in_specs=[pl.BlockSpec(memory_space=pltpu.VMEM)] * 7,
        out_specs=(pl.BlockSpec(memory_space=pltpu.VMEM),) * 2,
        scratch_shapes=list(scratch.values()),
        compiler_params=pltpu.CompilerParams(
            collective_id=0, has_side_effects=True, vmem_limit_bytes=63 << 20),
    )(wall_owner.reshape(segs // seg, seg), wall_row.reshape(segs // seg, seg),
      heat_capacity.reshape(1, channels), inlet_temp.reshape(1, channels),
      conductance, solid_start, heat_gen)


def solution(mesh):
    placed = (
        P(None, "flow", "span"),
        P(None, "flow", "span"),
        P("span", "flow"),
        P("span"),
        P("span"),
        P(("flow", "span"), None),
        P(("flow", "span"), None),
    )
    return jax.shard_map(
        body,
        mesh=mesh,
        in_specs=placed,
        out_specs=(P(None, "flow", "span"), P("span", "flow")),
        check_vma=False,
    )
```

time: 132 us -> 99.8 us (0.76)
  waiting for transfers between devices: 25.1 us -> 0 us
  Pallas kernels: 81.4 us -> 96 us
  between operations: 14.1 us -> 0.65 us
  local copies, waits for them, and re-layouts: 9.5 us -> 3 us
  other arithmetic: 1.96 us -> 0 us
    all_gather x1 -> x0, waiting for transfers between devices: 25.1 us -> none  [body(): packed = lax.all_gather(packed, 'flow')]
    pallas_call x1, Pallas kernels: 81.4 us -> 96 us  [body(): pl.pallas_call(run, out_shape=(jax.ShapeDtypeStruct(solid_start.shape, F3...]
    reshape x5 -> x0, local copies, waits for them, and re-layouts: 3.69 us -> none  [the longest x1 1.31 us: body(): jnp.transpose(cond, (3, 2, 0, 1)).reshape(seg, count * flow * channels)]
    unnamed x3 -> x4, local copies, waits for them, and re-layouts: 0.97 us -> 3 us
    pallas_call x1 -> x0, local copies, waits for them, and re-layouts: 1.64 us -> none  [body(): pl.pallas_call(run, out_shape=(jax.ShapeDtypeStruct(solid_start.shape, F3...]
    another operation x4 -> x0, local copies, waits for them, and re-layouts: 1.48 us -> none  [the longest x1 0.66 us: body(): jnp.tile(heat_capacity, flow)]
  transfers between devices with their start and end apart: 1 -> 0, of which waited for: 1 -> 0; matrix products, arithmetic and copies ran while one was open for 2% -> 0% of each run, Pallas kernels for 0% -> 0%
where the time goes in v1:
time: 99.8 us; the launch traced here: 99.6 us
  Pallas kernels  96 us (96%)
  local copies, waits for them, and re-layouts  3 us (3%)
    pallas_call x1, Pallas kernels, body(): pl.pallas_call(run, out_shape=(jax.ShapeDtypeStruct(solid_start.shape, F3...  96 us
    unnamed x4, local copies, waits for them, and re-layouts  3 us

profile of v1, /device:TPU:0, one launch (start us, length us, event | category | flops | bytes accessed | tf_op | source)
XLA Modules:
  0.0 99.6 jit_solution(6734119883380570860)
XLA Ops:
  0.6 96.0 %shard_map.86 = (f32[32,64,128]{2,1,0:T(8,128)}, f32[16,2048]{1,0:T(8,128)}) custom-call(s32[2,128]{1,0:T(2,128)} %bitcast.4, s32[2,128]{1,0:T(2,128)} %bitcast.5, f32[1,16]{1,0:T(1,128)} %bitcast.6, f32[1,16]{1,0:T(1,128)} %bitcast.7, f32[16,2048]{1,0:T(8,128)} %refs_4_.1, f32[32,64,128]{2,1,0:T(8,128)} %refs_5_.1, f32[32,64,128]{2,1,0:T(8,128)} %refs_6_.1), custom_call_target="tpu_custom_call" | custom-call | tf_op jit(solution)/shard_map/pallas_call | solution.py:542
  96.6 0.0 copy-start
  96.6 2.3 %copy.11 = f32[32,64,128]{2,1,0:T(8,128)} copy(f32[32,64,128]{2,1,0:T(8,128)} %get-tuple-element.4) | data formatting | bytes 2097152
  99.0 0.0 copy-done
  99.0 0.7 copy.12
Async XLA Ops:
  96.6 2.4 %copy-start = (f32[16,2048]{1,0:T(8,128)S(1)}, f32[16,2048]{1,0:T(8,128)}, u32[]{:S(2)}) copy-start(f32[16,2048]{1,0:T(8,128)} %get-tuple-element.5) | copy-start | bytes 393220

commit v2 on v1

--- a/solution.py
+++ b/solution.py
@@ -6,6 +6,7 @@
 from jax.sharding import PartitionSpec as P
 
 STEPS = 10
+PARTS = 4
 KAPPA = 0.16
 MESH = pl.DeviceIdType.MESH
 F32 = jnp.float32
@@ -27,6 +28,7 @@
     tiles = block // 8
     lines = cells // 8
     packs = -(-lines // (seg // 2))
+    deep = layers // PARTS
     me = lax.axis_index("flow")
     at = lax.axis_index("span")
     mate = me + 1 - 2 * lax.rem(me, 2)
@@ -47,8 +49,9 @@
 
     kinds = (
         (s.idx_own, lambda f: s.idx.at[f]),
-        (start_ref.at[pl.ds(0, 2)], lambda f: s.first.at[f]),
+        (start_ref.at[0], lambda f: s.plane.at[0, f]),
         (cond_ref, lambda f: s.gain.at[f]),
+        (start_ref.at[1], lambda f: s.one.at[0, f]),
         (gen_ref.at[0], lambda f: s.gen0.at[f]),
     )
 
@@ -66,26 +69,37 @@
         origin = lax.rem(me + flow - 2 * hop, flow)
         return remote(dst(origin), dst(origin), s.once_send.at[kind, 2 * hop], s.once_recv.at[kind, 2 * hop], (mate, at))
 
-    def layer_copy(slot, hop):
-        peer = lax.rem(me + hop, flow)
+    def one_direct(slot, hop):
+        to = lax.rem(me + 2 * hop, flow)
         return remote(s.one.at[slot, me], s.one.at[slot, me],
-                      s.one_send.at[hop - 1], s.one_recv.at[slot, hop - 1], (peer, at))
+                      s.one_send.at[2 * hop - 1], s.one_recv.at[slot, 2 * hop - 1], (to, at))
+
+    def one_to_mate(slot):
+        return remote(s.one.at[slot, me], s.one.at[slot, me],
+                      s.one_send.at[0], s.one_recv.at[slot, 0], (mate, at))
+
+    def one_relay(slot, hop):
+        origin = lax.rem(me + flow - 2 * hop, flow)
+        return remote(s.one.at[slot, origin], s.one.at[slot, origin],
+                      s.one_send.at[2 * hop], s.one_recv.at[slot, 2 * hop], (mate, at))
 
     def side_copy(slot, side):
         return remote(s.side_out, s.side_in.at[slot, 1 - side],
                       s.side_send.at[side], s.side_recv.at[slot, 1 - side], (me, at - 1 + 2 * side))
 
-    def rim_copy(slot, side):
-        return remote(s.rim_out, s.rim_in.at[slot, 1 - side],
-                      s.rim_send.at[side], s.rim_recv.at[slot, 1 - side], (me, at - 1 + 2 * side))
-
-    def col_copy(slot, side):
-        return remote(s.col_out, s.col_in.at[slot, 1 - side],
-                      s.col_send.at[side], s.col_recv.at[slot, 1 - side], (me, at - 1 + 2 * side))
-
-    def row_copy(slot, side):
-        return remote(s.row_out.at[side], s.row_in.at[slot, 1 - side],
-                      s.row_send.at[side], s.row_recv.at[slot, 1 - side], (me - 1 + 2 * side, at))
+    def col_copy(part):
+        def copy(slot, side):
+            return remote(s.col_out.at[part], s.col_in.at[slot, part, 1 - side],
+                          s.col_send.at[part, side], s.col_recv.at[slot, part, 1 - side], (me, at - 1 + 2 * side))
+        return copy
+
+    def row_copy(part):
+        rows = pl.ds(part * deep, deep)
+
+        def copy(slot, side):
+            return remote(s.row_out.at[side, rows], s.row_in.at[slot, 1 - side, rows],
+                          s.row_send.at[part, side], s.row_recv.at[slot, part, 1 - side], (me - 1 + 2 * side, at))
+        return copy
 
     def both(copy, pair_of, act):
         for side, there in enumerate(pair_of):
@@ -105,7 +119,6 @@
         both(copy, pair_of, lambda c, side: c(slot, 1 - side).wait_recv())
 
     s.side_in[...] = jnp.zeros_like(s.side_in)
-    s.rim_in[...] = jnp.zeros_like(s.rim_in)
     s.col_in[...] = jnp.zeros_like(s.col_in)
     s.row_in[...] = jnp.zeros_like(s.row_in)
     s.idx_own[...] = jnp.zeros_like(s.idx_own)
@@ -125,7 +138,8 @@
             direct(kind, hop).start()
         to_mate(kind).start()
     s.idx[me] = s.idx_own[...]
-    s.first[me] = start_ref[0:2]
+    s.plane[0, me] = start_ref[0]
+    s.one[0, me] = start_ref[1]
     s.gain[me] = cond_ref[...]
     s.gen0[me] = gen_ref[0]
 
@@ -143,17 +157,14 @@
         return jnp.concatenate(
             [pltpu.roll(marks[p], seg - 1 - 2 * k, 1) for p, k in (place(r) for r in range(tiles))], axis=0)
 
-    def rim_place(r):
-        return 0, r
-
     def col_place(z):
-        per_pack = seg // 2 // layers
-        return lambda r: (r // per_pack, z + layers * (r % per_pack))
+        per_pack = seg // 2 // deep
+        return lambda r: (r // per_pack, z % deep + deep * (r % per_pack))
 
     def side_place(b):
         return lambda r: divmod(b * tiles + r, seg // 2)
 
-    col_packs = s.col_out.shape[0]
+    col_packs = s.col_out.shape[1]
     empty = jnp.zeros((8, seg), F32)
 
     def around(c, low_row, high_row, halo):
@@ -162,7 +173,6 @@
         beside = beside + jnp.where(first_b, halo, pltpu.roll(c, 1, 1))
         return beside + jnp.where(last_b, halo, pltpu.roll(c, seg - 1, 1))
 
-    marks = [empty] * col_packs
     for side in range(2):
         s.row_out[side] = jnp.zeros_like(s.row_out[side])
     s.field[0, layers] = jnp.zeros((block, seg), F32)
@@ -172,19 +182,23 @@
         s.row_out[0, z:z + 1, :] = new[0:1, :]
         s.row_out[1, z:z + 1, :] = new[block - 1:block, :]
 
-    new = start_ref[1]
-    s.field[0, 1] = new
-    s.rim_out[...] = packed([empty], new, rim_place)[0]
-    start(rim_copy, 0, in_span)
-    for z in range(2, layers):
-        new = start_ref[z]
-        s.field[0, z] = new
-        note_rows(z, new)
-        marks = packed(marks, new, col_place(z))
-    for p in range(col_packs):
-        s.col_out[p] = marks[p]
-    start(row_copy, 0, in_flow)
-    start(col_copy, 0, in_span)
+    def members(part):
+        return range(max(1, part * deep), (part + 1) * deep)
+
+    def send_part(part, slot):
+        start(row_copy(part), slot, in_flow)
+        start(col_copy(part), slot, in_span)
+
+    for part in range(PARTS):
+        marks = [empty] * col_packs
+        for z in members(part):
+            new = start_ref[z]
+            s.field[0, z] = new
+            note_rows(z, new)
+            marks = packed(marks, new, col_place(z))
+        for p in range(col_packs):
+            s.col_out[part, p] = marks[p]
+        send_part(part, 0)
 
     mid = seg // 2 - 1
     i2 = lax.rem(lax.broadcasted_iota(jnp.int32, (2 * seg, 2 * seg), 0), seg)
@@ -205,30 +219,22 @@
 
     capacity, inlet = column(cap_ref), column(inlet_ref)
 
-    def arrivals(kind, i):
-        hop = i // 2
-        odd = lax.rem(i, 2) == 1
-
-        @pl.when(jnp.logical_and(jnp.logical_not(odd), i > 0))
-        def _():
-            direct(kind, hop).wait_recv()
-            relay(kind, hop).start()
-
-        @pl.when(i == 1)
-        def _():
-            to_mate(kind).wait_recv()
-
-        @pl.when(jnp.logical_and(odd, i > 1))
-        def _():
+    def hand_on(kind, hop):
+        direct(kind, hop).wait_recv()
+        relay(kind, hop).start()
+
+    def pass_on(kind):
+        for hop in range(1, half):
+            hand_on(kind, hop)
+
+    def take_in(kind):
+        to_mate(kind).wait_recv()
+        for hop in range(1, half):
             relay(kind, hop).wait_recv()
 
-    def gather_kind(kind):
-        def body(i, carry):
-            arrivals(kind, i)
-            return carry
-        lax.fori_loop(0, flow, body, 0)
-
-    gather_kind(0)
+    pass_on(0)
+    pass_on(1)
+    take_in(0)
     share = seg // count
     lane_i = lax.broadcasted_iota(jnp.int32, (channels, seg), 1) // count
     chan_i = lax.rem(lax.broadcasted_iota(jnp.int32, (channels, seg), 0), share)
@@ -287,14 +293,8 @@
         return jnp.concatenate(
             [jnp.where(rows == s.along[t:t + 1, :], 1.0, 0.0).astype(BF16) for t in range(t0, t0 + group)], axis=1)
 
-    gather_kind(1)
-
-    def place_first(f, carry):
-        s.plane[0, f] = s.first[f, 0]
-        s.one[0, f] = s.first[f, 1]
-        return carry
-
-    lax.fori_loop(0, flow, place_first, 0)
+    take_in(1)
+
     side_marks = [empty] * packs
     for b in range(flow):
         c = s.plane[0, b]
@@ -310,13 +310,25 @@
         return ref[:, :, t * seg:(t + 1) * seg].reshape(width, seg)
 
     def constants(i, carry):
-        arrivals(2, i)
-        hop = i // 2
+        own_core = jnp.logical_and(i >= 2, i <= half)
+        hop = jnp.where(i < 2, 0, jnp.where(i <= half, i - 1, i - half))
         from_me = lax.rem(me + flow - 2 * hop, flow)
         from_mate = lax.rem(mate + flow - 2 * hop, flow)
-        f = jnp.where(lax.rem(i, 2) == 0, from_me, from_mate)
-
-        @pl.when(jnp.logical_and(lax.rem(i, 2) == 0, i > 0))
+        f = jnp.where(jnp.logical_or(i == 0, own_core), from_me, from_mate)
+
+        @pl.when(i == 1)
+        def _():
+            to_mate(2).wait_recv()
+
+        @pl.when(own_core)
+        def _():
+            hand_on(2, hop)
+
+        @pl.when(i > half)
+        def _():
+            relay(2, hop).wait_recv()
+
+        @pl.when(own_core)
         def _():
             relay(2, hop).wait_send()
 
@@ -343,12 +355,10 @@
         return carry
 
     lax.fori_loop(0, flow, constants, 0)
-    gather_kind(3)
-
-    def coolant():
+
+    def march(run, first_t, last_t):
         base = s.base[...]
-        run = jnp.zeros((width, seg), F32)
-        for t0 in range(0, count, group):
+        for t0 in range(first_t, last_t, group):
             found = jnp.dot(take_rows(t0), base, preferred_element_type=F32)
             w = found[:, :seg] + found[:, seg:]
             gains = jnp.concatenate([chunk(s.gain, t) for t in range(t0, t0 + group)], axis=0)
@@ -361,6 +371,9 @@
                 s.part[t] = sums[rows, :seg]
                 s.run[t] = run
                 run = chunk(s.rear, t) * (sums[rows, seg:] + chunk(s.fore, t) * run)
+        return run
+
+    def heats(run):
         enter = inlet
         for f in range(flow):
             s.enter[f] = enter
@@ -374,75 +387,113 @@
                 s.heat[t * width:(t + 1) * width, 0:seg] = hi
                 s.heat[t * width:(t + 1) * width, seg:2 * seg] = lo
 
-    def sinks(b):
-        total = jnp.zeros((block, 2 * seg), F32)
-        for t0 in range(0, count, group):
-            total = total + jnp.dot(give_rows(t0, b), s.heat[t0 * width:(t0 + group) * width, :],
-                                    preferred_element_type=F32)
-        return total[:, :seg] + total[:, seg:]
-
-    def step(turn, carry):
-        slot, later = lax.rem(turn, 2), lax.rem(turn + 1, 2)
-        held, next_held = lax.rem(turn, 4), lax.rem(turn + 1, 4)
-        more = turn < STEPS - 1
-
-        @pl.when(turn > 0)
-        def _():
-            layer_copy(held, 1).wait_recv()
-            if flow > 2:
-                layer_copy(held, flow - 1).wait_recv()
-            for hop in range(1, flow):
-                layer_copy(held, hop).wait_send()
-        arrived(rim_copy, slot, in_span)
-        sent(rim_copy, slot, in_span)
-        c = s.field[slot, 1]
-        low = s.one[held, jnp.maximum(me - 1, 0), block - 1:block, :]
-        high = s.one[held, jnp.minimum(me + 1, flow - 1), 0:1, :]
-        halo = unpacked([merged(s.rim_in[slot, 0], s.rim_in[slot, 1])], rim_place)
-        beside = around(c, jnp.where(before, low, 0.0), jnp.where(after, high, 0.0), halo)
-        beside = beside + s.plane[slot, me] + s.field[slot, 2]
-        new = c + KAPPA * (beside - 6.0 * c) + gen_ref[1]
-        s.field[later, 1] = new
-        s.one[next_held, me] = new
-        s.rim_out[...] = packed([empty], new, rim_place)[0]
-
-        @pl.when(more)
-        def _():
-            for hop in range(1, flow):
-                layer_copy(next_held, hop).start()
-        @pl.when(more)
-        def _():
-            start(rim_copy, later, in_span)
-
-        coolant()
-
-        arrived(row_copy, slot, in_flow)
-        sent(row_copy, slot, in_flow)
-        arrived(col_copy, slot, in_span)
-        sent(col_copy, slot, in_span)
+    def sinks():
+        if keep:
+            total = jnp.dot(s.give[...], s.heat[...], preferred_element_type=F32)
+            s.sink[...] = total[:, :seg] + total[:, seg:]
+            return
+        for b in range(flow):
+            total = jnp.zeros((block, 2 * seg), F32)
+            for t0 in range(0, count, group):
+                total = total + jnp.dot(give_rows(t0, b), s.heat[t0 * width:(t0 + group) * width, :],
+                                        preferred_element_type=F32)
+            s.sink[b * block:(b + 1) * block, :] = total[:, :seg] + total[:, seg:]
+
+    def await_part(part, slot):
+        arrived(row_copy(part), slot, in_flow)
+        sent(row_copy(part), slot, in_flow)
+        arrived(col_copy(part), slot, in_span)
+        sent(col_copy(part), slot, in_span)
+
+    def conduct(part, slot, later):
         marks = [empty] * col_packs
-        halos = [merged(s.col_in[slot, 0, p], s.col_in[slot, 1, p]) for p in range(col_packs)]
-        for z in range(2, layers):
+        halos = [merged(s.col_in[slot, part, 0, p], s.col_in[slot, part, 1, p]) for p in range(col_packs)]
+        for z in members(part):
             c = s.field[slot, z]
             beside = around(c, s.row_in[slot, 0, z:z + 1, :], s.row_in[slot, 1, z:z + 1, :],
                             unpacked(halos, col_place(z)))
-            beside = beside + s.field[slot, z - 1] + s.field[slot, z + 1]
+            under = s.plane[slot, me] if z == 1 else s.field[slot, z - 1]
+            beside = beside + under + s.field[slot, z + 1]
             new = c + KAPPA * (beside - 6.0 * c) + gen_ref[z]
             s.field[later, z] = new
             note_rows(z, new)
             marks = packed(marks, new, col_place(z))
         for p in range(col_packs):
-            s.col_out[p] = marks[p]
+            s.col_out[part, p] = marks[p]
+
+    def step(turn, carry):
+        slot, later = lax.rem(turn, 2), lax.rem(turn + 1, 2)
+        held, next_held = lax.rem(turn, 4), lax.rem(turn + 1, 4)
+        more = turn < STEPS - 1
+
+        await_part(0, slot)
+        run = march(jnp.zeros((width, seg), F32), 0, count // 2)
+        conduct(0, slot, later)
+
+        @pl.when(turn > 0)
+        def _():
+            for hop in range(1, half):
+                one_direct(held, hop).wait_send()
+            one_to_mate(held).wait_send()
+
+        @pl.when(turn > 1)
+        def _():
+            for hop in range(1, half):
+                one_relay(held, hop).wait_send()
+        s.one[next_held, me] = s.field[later, 1]
 
         @pl.when(more)
         def _():
-            start(row_copy, later, in_flow)
-            start(col_copy, later, in_span)
+            send_part(0, later)
+            for hop in range(1, half):
+                one_direct(next_held, hop).start()
+            one_to_mate(next_held).start()
+        await_part(1, slot)
+        run = march(run, count // 2, count)
+        conduct(1, slot, later)
 
         @pl.when(turn > 0)
         def _():
-            for hop in range(2, flow - 1):
-                layer_copy(held, hop).wait_recv()
+            for hop in range(1, half):
+                one_direct(held, hop).wait_recv()
+                one_relay(held, hop).start()
+
+        @pl.when(turn == 0)
+        def _():
+            pass_on(3)
+            pass_on(4)
+
+        @pl.when(more)
+        def _():
+            send_part(1, later)
+        await_part(2, slot)
+        heats(run)
+        conduct(2, slot, later)
+
+        @pl.when(more)
+        def _():
+            send_part(2, later)
+        await_part(3, slot)
+        sinks()
+        conduct(3, slot, later)
+
+        @pl.when(more)
+        def _():
+            send_part(3, later)
+
+        @pl.when(turn == 0)
+        def _():
+            take_in(3)
+            take_in(4)
+            for hop in range(1, half):
+                relay(1, hop).wait_send()
+                relay(3, hop).wait_send()
+
+        @pl.when(turn > 0)
+        def _():
+            one_to_mate(held).wait_recv()
+            for hop in range(1, half):
+                one_relay(held, hop).wait_recv()
         arrived(side_copy, slot, in_span)
         sent(side_copy, slot, in_span)
         halos = [merged(s.side_in[slot, 0, p], s.side_in[slot, 1, p]) for p in range(packs)]
@@ -452,7 +503,7 @@
             low = s.plane[slot, b - 1, block - 1:block, :] if b else jnp.zeros((1, seg), F32)
             high = s.plane[slot, b + 1, 0:1, :] if b < flow - 1 else jnp.zeros((1, seg), F32)
             beside = around(c, low, high, unpacked(halos, side_place(b))) + s.one[held, b]
-            new = c + KAPPA * (beside - 6.0 * c) + s.gen0[b] - sinks(b)
+            new = c + KAPPA * (beside - 6.0 * c) + s.gen0[b] - s.sink[b * block:(b + 1) * block, :]
             s.plane[later, b] = new
             side_marks = packed(side_marks, new, side_place(b))
             hi, lo = split(new)
@@ -470,9 +521,11 @@
     for kind in range(len(kinds)):
         for hop in range(1, half):
             direct(kind, hop).wait_send()
-            if kind != 2:
+            if kind in (0, 4):
                 relay(kind, hop).wait_send()
         to_mate(kind).wait_send()
+    for hop in range(1, half):
+        one_relay(0, hop).wait_send()
     last = STEPS % 2
     solid_out[0] = s.plane[last, me]
     for z in range(1, layers):
@@ -503,19 +556,19 @@
     keep = cells * total * 4 <= (8 << 20)
     group = max(1, 512 // width)
     packs = -(-lines // (seg // 2))
-    col_packs = -(-(block // 8) // (seg // 2 // layers))
+    col_packs = -(-(block // 8) // (seg // 2 // (layers // PARTS)))
     dims = (flow, span, layers, block, seg, channels, count, group, keep)
     vm = pltpu.VMEM
     dma = pltpu.SemaphoreType.DMA
     march = vm((flow, channels, stations), F32)
     parts = vm((count, width, seg), F32)
     scratch = dict(
-        idx_own=vm((8, seg), F32), idx=vm((flow, 8, seg), F32), first=vm((flow, 2, block, seg), F32),
+        idx_own=vm((8, seg), F32), idx=vm((flow, 8, seg), F32),
         gen0=vm((flow, block, seg), F32), one=vm((4, flow, block, seg), F32),
         plane=vm((2, flow, block, seg), F32), field=vm((2, layers + 1, block, seg), F32),
         side_out=vm((packs, 8, seg), F32), side_in=vm((2, 2, packs, 8, seg), F32),
-        rim_out=vm((8, seg), F32), rim_in=vm((2, 2, 8, seg), F32),
-        col_out=vm((col_packs, 8, seg), F32), col_in=vm((2, 2, col_packs, 8, seg), F32),
+        sink=vm((cells, seg), F32),
+        col_out=vm((PARTS, col_packs, 8, seg), F32), col_in=vm((2, PARTS, 2, col_packs, 8, seg), F32),
         row_out=vm((2, layers, seg), F32), row_in=vm((2, 2, layers, seg), F32),
         tri=vm((2 * seg, 2 * seg), BF16), seats=vm((flow, channels, 2 * seg), BF16),
         along=vm((count, width), F32),
@@ -524,10 +577,11 @@
         gain=march, fall=march, heat_of=march, fore=march, rear=march, reach=march,
         whole=vm((flow, channels, seg), F32), enter=vm((flow, channels, seg), F32),
         wall=parts, part=parts, run=parts,
-        once_send=dma((4, flow - 1)), once_recv=dma((4, flow - 1)),
+        once_send=dma((5, flow - 1)), once_recv=dma((5, flow - 1)),
         one_send=dma((flow - 1,)), one_recv=dma((4, flow - 1)),
-        side_send=dma((2,)), side_recv=dma((2, 2)), rim_send=dma((2,)), rim_recv=dma((2, 2)),
-        col_send=dma((2,)), col_recv=dma((2, 2)), row_send=dma((2,)), row_recv=dma((2, 2)),
+        side_send=dma((2,)), side_recv=dma((2, 2)),
+        col_send=dma((PARTS, 2)), col_recv=dma((2, PARTS, 2)),
+        row_send=dma((PARTS, 2)), row_recv=dma((2, PARTS, 2)),
     )
     if keep:
         scratch["give"] = vm((cells, total), BF16)

time: 99.8 us -> 78.4 us (0.79)
  Pallas kernels: 96 us -> 74.6 us
    pallas_call x1, Pallas kernels: 96 us -> 74.6 us  [body(): pl.pallas_call(run, out_shape=(jax.ShapeDtypeStruct(solid_start.shape, F3...]
where the time goes in v2:
time: 78.4 us; the launch traced here: 78.3 us
  Pallas kernels  74.6 us (95%)
  local copies, waits for them, and re-layouts  3 us (4%)
    pallas_call x1, Pallas kernels, body(): pl.pallas_call(run, out_shape=(jax.ShapeDtypeStruct(solid_start.shape, F3...  74.6 us
    unnamed x4, local copies, waits for them, and re-layouts  3 us

profile of v2, /device:TPU:0, one launch (start us, length us, event | category | flops | bytes accessed | tf_op | source)
XLA Modules:
  0.0 78.3 jit_solution(196111209847494697)
XLA Ops:
  0.6 74.6 %shard_map.86 = (f32[32,64,128]{2,1,0:T(8,128)}, f32[16,2048]{1,0:T(8,128)}) custom-call(s32[2,128]{1,0:T(2,128)} %bitcast.4, s32[2,128]{1,0:T(2,128)} %bitcast.5, f32[1,16]{1,0:T(1,128)} %bitcast.6, f32[1,16]{1,0:T(1,128)} %bitcast.7, f32[16,2048]{1,0:T(8,128)} %refs_4_.1, f32[32,64,128]{2,1,0:T(8,128)} %refs_5_.1, f32[32,64,128]{2,1,0:T(8,128)} %refs_6_.1), custom_call_target="tpu_custom_call" | custom-call | tf_op jit(solution)/shard_map/pallas_call | solution.py:596
  75.2 0.0 copy-start
  75.2 2.3 %copy.11 = f32[32,64,128]{2,1,0:T(8,128)} copy(f32[32,64,128]{2,1,0:T(8,128)} %get-tuple-element.4) | data formatting | bytes 2097152
  77.6 0.0 copy-done
  77.6 0.7 copy.12
Async XLA Ops:
  75.2 2.4 %copy-start = (f32[16,2048]{1,0:T(8,128)S(1)}, f32[16,2048]{1,0:T(8,128)}, u32[]{:S(2)}) copy-start(f32[16,2048]{1,0:T(8,128)} %get-tuple-element.5) | copy-start | bytes 393220

commit v3 on v2

--- a/solution.py
+++ b/solution.py
@@ -349,7 +349,7 @@
             s.heat_of[f, :, cols] = (jnp.exp(kt) - 1.0) * capacity
             s.fore[f, :, cols] = fore
             s.rear[f, :, cols] = rear
-            s.reach[f, :, cols] = run
+            s.reach[f, :, cols] = fore * run
             run = run * (fore * rear)
         s.whole[f] = run
         return carry
@@ -368,36 +368,41 @@
                 t = t0 + i
                 rows = slice(i * width, (i + 1) * width)
                 s.wall[t] = w[rows]
-                s.part[t] = sums[rows, :seg]
-                s.run[t] = run
-                run = chunk(s.rear, t) * (sums[rows, seg:] + chunk(s.fore, t) * run)
+                into = chunk(s.fore, t) * run
+                s.part[t] = sums[rows, :seg] + into
+                run = chunk(s.rear, t) * (sums[rows, seg:] + into)
         return run
 
-    def heats(run):
+    def carries(run):
         enter = inlet
         for f in range(flow):
             s.enter[f] = enter
             enter = run[f * channels:(f + 1) * channels] + s.whole[f] * enter
+
+    def heats(first_t, last_t):
         enter = s.enter[...].reshape(width, seg)
-        for t0 in range(0, count, group):
-            for t in range(t0, t0 + group):
-                first = s.run[t] + chunk(s.reach, t) * enter
-                cool = chunk(s.fall, t) * (s.part[t] + chunk(s.fore, t) * first)
-                hi, lo = split(chunk(s.heat_of, t) * (s.wall[t] - cool))
-                s.heat[t * width:(t + 1) * width, 0:seg] = hi
-                s.heat[t * width:(t + 1) * width, seg:2 * seg] = lo
-
-    def sinks():
+        for t in range(first_t, last_t):
+            cool = chunk(s.fall, t) * (s.part[t] + chunk(s.reach, t) * enter)
+            hi, lo = split(chunk(s.heat_of, t) * (s.wall[t] - cool))
+            s.heat[t * width:(t + 1) * width, 0:seg] = hi
+            s.heat[t * width:(t + 1) * width, seg:2 * seg] = lo
+
+    def sinks(b, first_t, last_t):
         if keep:
-            total = jnp.dot(s.give[...], s.heat[...], preferred_element_type=F32)
-            s.sink[...] = total[:, :seg] + total[:, seg:]
-            return
-        for b in range(flow):
+            cols = slice(first_t * width, last_t * width)
+            total = jnp.dot(s.give[:, cols] if b is None else s.give[b * block:(b + 1) * block, cols],
+                            s.heat[cols, :], preferred_element_type=F32)
+        else:
             total = jnp.zeros((block, 2 * seg), F32)
-            for t0 in range(0, count, group):
+            for t0 in range(first_t, last_t, group):
                 total = total + jnp.dot(give_rows(t0, b), s.heat[t0 * width:(t0 + group) * width, :],
                                         preferred_element_type=F32)
-            s.sink[b * block:(b + 1) * block, :] = total[:, :seg] + total[:, seg:]
+        return total[:, :seg] + total[:, seg:]
+
+    def all_sinks(first_t, last_t):
+        if keep:
+            return sinks(None, first_t, last_t)
+        return jnp.concatenate([sinks(b, first_t, last_t) for b in range(flow)], axis=0)
 
     def await_part(part, slot):
         arrived(row_copy(part), slot, in_flow)
@@ -467,14 +472,16 @@
         def _():
             send_part(1, later)
         await_part(2, slot)
-        heats(run)
+        carries(run)
+        heats(0, count // 2)
         conduct(2, slot, later)
 
         @pl.when(more)
         def _():
             send_part(2, later)
         await_part(3, slot)
-        sinks()
+        s.sink[...] = all_sinks(0, count // 2)
+        heats(count // 2, count)
         conduct(3, slot, later)
 
         @pl.when(more)
@@ -498,12 +505,14 @@
         sent(side_copy, slot, in_span)
         halos = [merged(s.side_in[slot, 0, p], s.side_in[slot, 1, p]) for p in range(packs)]
         side_marks = [empty] * packs
+        rest = all_sinks(count // 2, count)
         for b in range(flow):
+            rows = slice(b * block, (b + 1) * block)
             c = s.plane[slot, b]
             low = s.plane[slot, b - 1, block - 1:block, :] if b else jnp.zeros((1, seg), F32)
             high = s.plane[slot, b + 1, 0:1, :] if b < flow - 1 else jnp.zeros((1, seg), F32)
             beside = around(c, low, high, unpacked(halos, side_place(b))) + s.one[held, b]
-            new = c + KAPPA * (beside - 6.0 * c) + s.gen0[b] - s.sink[b * block:(b + 1) * block, :]
+            new = c + KAPPA * (beside - 6.0 * c) + s.gen0[b] - (s.sink[rows, :] + rest[rows])
             s.plane[later, b] = new
             side_marks = packed(side_marks, new, side_place(b))
             hi, lo = split(new)
@@ -533,8 +542,7 @@
     rows = pl.ds(pl.multiple_of(me * channels, channels), channels)
     for t in range(count):
         cols = slice(t * seg, (t + 1) * seg)
-        first = s.run[t, rows, :] + s.reach[me, :, cols] * s.enter[me]
-        cool_out[:, cols] = s.fall[me, :, cols] * (s.part[t, rows, :] + s.fore[me, :, cols] * first)
+        cool_out[:, cols] = s.fall[me, :, cols] * (s.part[t, rows, :] + s.reach[me, :, cols] * s.enter[me])
 
 
 class Scratch:
@@ -576,7 +584,7 @@
         base=vm((cells, 2 * seg), BF16), heat=vm((total, 2 * seg), BF16),
         gain=march, fall=march, heat_of=march, fore=march, rear=march, reach=march,
         whole=vm((flow, channels, seg), F32), enter=vm((flow, channels, seg), F32),
-        wall=parts, part=parts, run=parts,
+        wall=parts, part=parts,
         once_send=dma((5, flow - 1)), once_recv=dma((5, flow - 1)),
         one_send=dma((flow - 1,)), one_recv=dma((4, flow - 1)),
         side_send=dma((2,)), side_recv=dma((2, 2)),

time: 78.4 us -> 74.7 us (0.953)
  Pallas kernels: 74.6 us -> 70.9 us
    pallas_call x1, Pallas kernels: 74.6 us -> 70.9 us  [body(): pl.pallas_call(run, out_shape=(jax.ShapeDtypeStruct(solid_start.shape, F3...]
where the time goes in v3:
time: 74.7 us; the launch traced here: 74.6 us
  Pallas kernels  70.9 us (95%)
  local copies, waits for them, and re-layouts  3 us (4%)
    pallas_call x1, Pallas kernels, body(): pl.pallas_call(run, out_shape=(jax.ShapeDtypeStruct(solid_start.shape, F3...  70.9 us
    unnamed x4, local copies, waits for them, and re-layouts  3 us

profile of v3, /device:TPU:0, one launch (start us, length us, event | category | flops | bytes accessed | tf_op | source)
XLA Modules:
  0.0 74.6 jit_solution(12575501794078341040)
XLA Ops:
  0.6 70.9 %shard_map.86 = (f32[32,64,128]{2,1,0:T(8,128)}, f32[16,2048]{1,0:T(8,128)}) custom-call(s32[2,128]{1,0:T(2,128)} %bitcast.4, s32[2,128]{1,0:T(2,128)} %bitcast.5, f32[1,16]{1,0:T(1,128)} %bitcast.6, f32[1,16]{1,0:T(1,128)} %bitcast.7, f32[16,2048]{1,0:T(8,128)} %refs_4_.1, f32[32,64,128]{2,1,0:T(8,128)} %refs_5_.1, f32[32,64,128]{2,1,0:T(8,128)} %refs_6_.1), custom_call_target="tpu_custom_call" | custom-call | tf_op jit(solution)/shard_map/pallas_call | solution.py:604
  71.5 0.0 copy-start
  71.6 2.3 %copy.11 = f32[32,64,128]{2,1,0:T(8,128)} copy(f32[32,64,128]{2,1,0:T(8,128)} %get-tuple-element.4) | data formatting | bytes 2097152
  73.9 0.0 copy-done
  73.9 0.7 copy.12
Async XLA Ops:
  71.5 2.4 %copy-start = (f32[16,2048]{1,0:T(8,128)S(1)}, f32[16,2048]{1,0:T(8,128)}, u32[]{:S(2)}) copy-start(f32[16,2048]{1,0:T(8,128)} %get-tuple-element.5) | copy-start | bytes 393220

commit v4 on v3

--- a/solution.py
+++ b/solution.py
@@ -603,13 +603,14 @@
 
     return pl.pallas_call(
         run,
-        out_shape=(jax.ShapeDtypeStruct(solid_start.shape, F32),
-                   jax.ShapeDtypeStruct(conductance.shape, F32)),
+        out_shape=tuple(
+            vm(x.shape, F32) if keep else jax.ShapeDtypeStruct(x.shape, F32)
+            for x in (solid_start, conductance)),
         in_specs=[pl.BlockSpec(memory_space=pltpu.VMEM)] * 7,
         out_specs=(pl.BlockSpec(memory_space=pltpu.VMEM),) * 2,
         scratch_shapes=list(scratch.values()),
         compiler_params=pltpu.CompilerParams(
-            collective_id=0, has_side_effects=True, vmem_limit_bytes=63 << 20),
+            collective_id=0, has_side_effects=True, vmem_limit_bytes=(62 if keep else 63) << 20),
     )(wall_owner.reshape(segs // seg, seg), wall_row.reshape(segs // seg, seg),
       heat_capacity.reshape(1, channels), inlet_temp.reshape(1, channels),
       conductance, solid_start, heat_gen)

time: 74.7 us -> 72.3 us (0.968)
  local copies, waits for them, and re-layouts: 3 us -> 1.63 us
  Pallas kernels: 70.9 us -> 69.9 us
    unnamed x4 -> x2, local copies, waits for them, and re-layouts: 3 us -> 1.63 us
    pallas_call x1, Pallas kernels: 70.9 us -> 69.9 us  [body(): pl.pallas_call(run, out_shape=tuple((vm(x.shape, F32) if keep else jax.Sh...]
where the time goes in v4:
time: 72.3 us; the launch traced here: 72.2 us
  Pallas kernels  69.9 us (97%)
  local copies, waits for them, and re-layouts  1.63 us (2%)
    pallas_call x1, Pallas kernels, body(): pl.pallas_call(run, out_shape=tuple((vm(x.shape, F32) if keep else jax.Sh...  69.9 us
    unnamed x2, local copies, waits for them, and re-layouts  1.63 us

profile of v4, /device:TPU:0, one launch (start us, length us, event | category | flops | bytes accessed | tf_op | source)
XLA Modules:
  0.0 72.2 jit_solution(16259809365818147434)
XLA Ops:
  0.6 69.9 %shard_map.86 = (f32[32,64,128]{2,1,0:T(8,128)S(1)}, f32[16,2048]{1,0:T(8,128)S(1)}) custom-call(s32[2,128]{1,0:T(2,128)} %bitcast.4, s32[2,128]{1,0:T(2,128)} %bitcast.5, f32[1,16]{1,0:T(1,128)} %bitcast.6, f32[1,16]{1,0:T(1,128)} %bitcast.7, f32[16,2048]{1,0:T(8,128)} %refs_4_.1, f32[32,64,128]{2,1,0:T(8,128)} %refs_5_.1, f32[32,64,128]{2,1,0:T(8,128)} %refs_6_.1), custom_call_target="tpu_custom_call" | custom-call | tf_op jit(solution)/shard_map/pallas_call | solution.py:604
  70.5 1.0 %copy.11 = f32[32,64,128]{2,1,0:T(8,128)} copy(f32[32,64,128]{2,1,0:T(8,128)S(1)} %get-tuple-element.2) | data formatting | bytes 2097152
  71.5 0.7 copy.12
